TPU v7x, 32 devices: a whole 2x2x4 slice. The times are simulated.
32 devices in a mesh: ep: 4 (over y, x), tp: 8 (over z, core).
Axes of the slice: x: 2, y: 2, z: 4, core: 2. Of those that a mesh axis runs over, the one named last changes fastest.
Arguments:
- tokens: bfloat16 [512, 6144], P('ep'), may hold values from -6 to 6
- expert_ids: int32 [512, 2], P('ep'), may hold values from 0 to 3, all different within a row; in each aligned block of 128 rows (0 to 127, 128 to 255, ...) at most 96 rows name the same one
- router: bfloat16 [6144, 4], replicated, may hold values from -0.078125 to 0.078125
- gate_weight: bfloat16 [4, 6144, 8192], P('ep', None, 'tp'), may hold values from -0.078125 to 0.078125
- up_weight: bfloat16 [4, 6144, 8192], P('ep', None, 'tp'), may hold values from -0.078125 to 0.078125
- down_weight: bfloat16 [4, 8192, 6144], P('ep', 'tp'), may hold values from -0.0625 to 0.0625
- keep_mask: int32 [512, 6144], P('ep'), may hold values 0 or 1
Outputs:
- layer_out: bfloat16 [512, 6144], P('ep')
Inputs may be any that keep to these rules, and one draw needn't show every extreme that they name: `expert_ids`: each row names two different experts. In the rows of one token block of 128 rows no expert is named more than 96 times, a bound that some block reaches.
All inputs are finite; a program needn't handle non-finite values. No bound on the sum of `keep_mask` on one device may be relied on, other than what follows from the above.
Results may differ from a plain program's by a relative error of at most 0.018.
Values may be sent and summed in bfloat16 or wider, within the bound.
A program may use at most 128 MiB of HBM per device.

v0:
```python
import functools

import jax
import jax.numpy as jnp
from jax import lax
from jax.experimental import pallas as pl
from jax.experimental.pallas import tpu as pltpu
from jax.sharding import PartitionSpec as P

MESH = pl.DeviceIdType.MESH


def flip(index, offset, count):
    out, bit = 0, 1
    while bit < count:
        out = out + ((index // bit + offset // bit) % 2) * bit
        bit *= 2
    return out


def kernel(
    n_ep, nz, slots_ref, comb_ref, gate_hbm, up_hbm, down_hbm, mask_hbm, out_ref,
    w_gate, w_up, w_down, mask, rows, hidden, pair_out, pair_in, mine, ep_out, ep_in,
    z_out, z_in, local_sem, disp_s, disp_r, fwd_s, fwd_r, pair_s, pair_r, ep_s, ep_r,
    z_s, z_r, gat_s, gat_r, gfw_s, gfw_r,
):
    ep, tp = lax.axis_index("ep"), lax.axis_index("tp")
    z, core = tp // 2, tp % 2
    partner = (ep, z * 2 + (1 - core))
    cap, width = rows.shape[1], rows.shape[2]
    toks = out_ref.shape[0]
    ff = w_gate.shape[1]
    half, piece = width // 2, width // (2 * nz)
    total_rows = n_ep * cap

    rounds = pair_in.shape[0] // nz
    sub = piece // rounds

    def cols(owner_core, owner_z, turn=None):
        if turn is None:
            return pl.ds(pl.multiple_of((owner_core * nz + owner_z) * piece, 128), piece)
        return pl.ds(pl.multiple_of((owner_core * nz + owner_z) * piece + turn * sub, 128), sub)

    my_half = pl.ds(pl.multiple_of(core * half, 128), half)

    load_own = pltpu.make_async_copy(slots_ref.at[ep], rows.at[0], local_sem.at[0])
    load_gate = pltpu.make_async_copy(gate_hbm, w_gate, local_sem.at[1])
    load_up = pltpu.make_async_copy(up_hbm, w_up, local_sem.at[2])
    load_down = pltpu.make_async_copy(down_hbm, w_down, local_sem.at[3])
    load_mask = pltpu.make_async_copy(mask_hbm.at[:, cols(core, z)], mask, local_sem.at[4])
    for load in (load_own, load_gate, load_up):
        load.start()

    barrier = pltpu.get_barrier_semaphore()
    peers = [(flip(ep, o, n_ep), tp) for o in range(1, n_ep)]
    peers += [(ep, ((z + s) % nz) * 2 + core) for s in range(1, nz)] + [partner]
    for peer in peers:
        pl.semaphore_signal(barrier, inc=1, device_id=peer, device_id_type=MESH)
    pl.semaphore_wait(barrier, len(peers))

    def remote(src, dst, send, recv, device):
        return pltpu.make_async_remote_copy(
            src_ref=src, dst_ref=dst, send_sem=send, recv_sem=recv,
            device_id=device, device_id_type=MESH,
        )

    started = []

    third = half // 3
    odd = z % 2
    z_pair = (ep, (z + 1 - 2 * odd) * 2 + core)

    def part(which):
        return pl.ds(pl.multiple_of(core * half + which * third, 128), third)

    shared, common, foreign = part(2 * odd), part(1), part(2 - 2 * odd)
    arrive, forward = {}, {}

    def send_rows(o, kind, at):
        peer = flip(ep, o, n_ep)
        copy = remote(slots_ref.at[peer, :, at], rows.at[o, :, at],
                      disp_s.at[kind, o], disp_r.at[kind, o], (peer, tp))
        copy.start()
        arrive[kind, o] = copy
        started.append(copy)

    def pass_on(o, kind, at):
        arrive[kind, o].wait_recv()
        if kind == 0:
            copy = remote(rows.at[o, :, at], rows.at[o, :, at],
                          disp_s.at[2, o], disp_r.at[2, o], z_pair)
            copy.start()
            arrive[2, o] = copy
            started.append(copy)
        copy = remote(rows.at[o, :, at], rows.at[o, :, at],
                      fwd_s.at[kind, o], fwd_r.at[kind, o], partner)
        copy.start()
        forward[kind, o] = copy
        started.append(copy)

    share_order = [n_ep - 1] + list(range(1, n_ep - 1))
    for o in share_order:
        send_rows(o, 0, shared)
    for o in range(1, n_ep):
        send_rows(o, 1, common)
    load_down.start()
    load_mask.start()
    for o in share_order:
        pass_on(o, 0, shared)

    tile = min(256, ff)
    phases = 2
    per = n_ep // phases
    for phase in range(phases):
        for o in range(phase * per, (phase + 1) * per):
            if o > 0:
                pass_on(o, 1, common)
                pass_on(o, 2, foreign)
        if phase == 0:
            load_own.wait()
            load_gate.wait()
            load_up.wait()
        for o in range(phase * per, (phase + 1) * per):
            if o > 0:
                for kind in range(3):
                    forward[kind, o].wait_recv()

        def up_step(t, carry):
            at = pl.ds(pl.multiple_of(t * tile, tile), tile)
            block = rows[phase * per:(phase + 1) * per].reshape(per * cap, width)
            gate = jnp.dot(block, w_gate[:, at], preferred_element_type=jnp.float32)
            up = jnp.dot(block, w_up[:, at], preferred_element_type=jnp.float32)
            hidden[phase * per * cap:(phase + 1) * per * cap, at] = (
                jax.nn.silu(gate) * up).astype(jnp.bfloat16)
            return carry

        lax.fori_loop(0, ff // tile, up_step, 0)

    load_down.wait()

    def pair_sum(s):
        pair[s].wait_recv()
        summed = (mine[s % 2].astype(jnp.float32) + pair_in[s].astype(jnp.float32)).astype(jnp.bfloat16)
        ep_in[s, 0:cap, :] = summed[0:cap]
        ep_out[s] = summed[cap:]
        for o in range(1, n_ep):
            copy = remote(ep_out.at[s, pl.ds((o - 1) * cap, cap), :], ep_in.at[s, pl.ds(o * cap, cap), :],
                          ep_s.at[s, o], ep_r.at[s, o], (flip(ep, o, n_ep), tp))
            copy.start()
            exchange[s].append(copy)
            started.append(copy)

    pair, exchange = [], [[] for _ in range(rounds * nz)]
    for s in range(rounds * nz):
        turn, owner = s // nz, (z + 1 + s % nz) % nz
        pair_out[s] = jnp.dot(hidden[...], w_down[:, cols(1 - core, owner, turn)],
                              preferred_element_type=jnp.float32).astype(jnp.bfloat16)
        copy = remote(pair_out.at[s], pair_in.at[s], pair_s.at[s], pair_r.at[s], partner)
        copy.start()
        pair.append(copy)
        started.append(copy)
        if s > 0:
            pair_sum(s - 1)
        mine[s % 2] = jnp.dot(hidden[...], w_down[:, cols(core, owner, turn)],
                              preferred_element_type=jnp.float32).astype(jnp.bfloat16)
    pair_sum(rounds * nz - 1)

    load_mask.wait()
    gather = {}
    passed = []

    def hand_over(turn):
        for s in range(1, nz):
            gather[turn, s].wait_recv()
            there = out_ref.at[:, cols(core, (z + nz - s) % nz, turn)]
            copy = remote(there, there, gfw_s.at[turn, s], gfw_r.at[turn, s], partner)
            copy.start()
            passed.append(copy)
            started.append(copy)

    for turn in range(rounds):
        reduce = []
        for s in range(nz):
            step = turn * nz + s
            owner = (z + 1 + s) % nz
            for copy in exchange[step]:
                copy.wait_recv()
            both = jnp.dot(comb_ref[...], ep_in[step], preferred_element_type=jnp.float32)
            token_sum = both[0:toks] + both[toks:]
            if s < nz - 1:
                z_out[turn, s] = token_sum.astype(jnp.bfloat16)
                copy = remote(z_out.at[turn, s], z_in.at[turn, s], z_s.at[turn, s], z_r.at[turn, s],
                              (ep, owner * 2 + core))
                copy.start()
                reduce.append(copy)
                started.append(copy)
        for s in range(nz - 1):
            reduce[s].wait_recv()
            token_sum = token_sum + z_in[turn, s].astype(jnp.float32)
        keep = mask[:, turn * sub:(turn + 1) * sub].astype(jnp.float32)
        out_ref[:, cols(core, z, turn)] = (token_sum * keep * 1.25).astype(jnp.bfloat16)
        here = out_ref.at[:, cols(core, z, turn)]
        for s in range(1, nz):
            copy = remote(here, here, gat_s.at[turn, s], gat_r.at[turn, s], (ep, ((z + s) % nz) * 2 + core))
            copy.start()
            gather[turn, s] = copy
            started.append(copy)
        copy = remote(here, here, gfw_s.at[turn, 0], gfw_r.at[turn, 0], partner)
        copy.start()
        passed.append(copy)
        started.append(copy)
        if turn > 0:
            hand_over(turn - 1)
    hand_over(rounds - 1)
    for copy in passed:
        copy.wait_recv()
    for copy in started:
        copy.wait_send()


def shards(n_ep, n_tp, tokens, expert_ids, router, gate_weight, up_weight, down_weight, keep_mask):
    experts = router.shape[1]
    toks, width = tokens.shape
    cap = 3 * toks // experts
    nz = n_tp // 2
    piece = width // n_tp
    total = experts * cap
    rounds = 3 if piece % 384 == 0 and piece > 384 else 1
    sub, steps = piece // rounds, rounds * nz
    logits = jnp.dot(tokens, router, preferred_element_type=jnp.float32)
    numbers = jnp.arange(experts, dtype=jnp.int32)
    onehot3 = expert_ids[:, :, None] == numbers[None, None, :]
    picked = jnp.sum(jnp.where(onehot3, logits[:, None, :], 0.0), axis=2)
    weight_first = jax.nn.sigmoid(picked[:, 0] - picked[:, 1])
    weight_second = jax.nn.sigmoid(picked[:, 1] - picked[:, 0])
    onehot = onehot3.astype(jnp.float32)
    named = onehot[:, 0] + onehot[:, 1]
    order = jnp.arange(toks, dtype=jnp.int32)
    before = (order[None, :] < order[:, None]).astype(jnp.bfloat16)
    ranks = jnp.dot(before, named.astype(jnp.bfloat16), preferred_element_type=jnp.float32)
    slot = jnp.sum(ranks[:, None, :] * onehot, axis=2).astype(jnp.int32)
    lines = jnp.arange(total, dtype=jnp.int32)
    place = expert_ids * cap + slot
    picker = ((place[None, :, 0] == lines[:, None]) | (place[None, :, 1] == lines[:, None])).astype(jnp.bfloat16)
    slots = jnp.dot(picker, tokens, preferred_element_type=jnp.float32).astype(jnp.bfloat16)
    slots = slots.reshape(experts, cap, width)
    turned = jnp.bitwise_xor(expert_ids, lax.axis_index("ep")) * cap + slot
    comb = (jnp.where(turned[:, 0:1] == lines[None, :], weight_first[:, None], 0.0)
            + jnp.where(turned[:, 1:2] == lines[None, :], weight_second[:, None], 0.0))
    high = lax.reduce_precision(comb, 8, 7)
    comb = jnp.concatenate([high, comb - high], axis=0).astype(jnp.bfloat16)
    w_gate, w_up, w_down = gate_weight[0], up_weight[0], down_weight[0]
    ff = w_gate.shape[1]
    vmem, hbm = pl.BlockSpec(memory_space=pltpu.VMEM), pl.BlockSpec(memory_space=pl.ANY)
    bf = jnp.bfloat16
    dma = pltpu.SemaphoreType.DMA
    return pl.pallas_call(
        functools.partial(kernel, n_ep, nz),
        out_shape=jax.ShapeDtypeStruct((toks, width), bf),
        in_specs=[vmem, vmem, hbm, hbm, hbm, hbm],
        out_specs=vmem,
        scratch_shapes=[
            pltpu.VMEM((width, ff), bf), pltpu.VMEM((width, ff), bf), pltpu.VMEM((ff, width), bf),
            pltpu.VMEM((toks, piece), jnp.int32),
            pltpu.VMEM((experts, cap, width), bf),
            pltpu.VMEM((total, ff), bf),
            pltpu.VMEM((steps, total, sub), bf), pltpu.VMEM((steps, total, sub), bf),
            pltpu.VMEM((2, total, sub), bf),
            pltpu.VMEM((steps, total - cap, sub), bf), pltpu.VMEM((steps, total, sub), bf),
            pltpu.VMEM((rounds, nz - 1, toks, sub), bf), pltpu.VMEM((rounds, nz - 1, toks, sub), bf),
            dma((5,)), dma((3, n_ep)), dma((3, n_ep)), dma((3, n_ep)), dma((3, n_ep)),
            dma((steps,)), dma((steps,)), dma((steps, n_ep)), dma((steps, n_ep)),
            dma((rounds, nz)), dma((rounds, nz)), dma((rounds, nz)), dma((rounds, nz)),
            dma((rounds, nz)), dma((rounds, nz)),
        ],
        compiler_params=pltpu.CompilerParams(
            collective_id=0, has_side_effects=True, vmem_limit_bytes=67043328),
    )(slots, comb, w_gate, w_up, w_down, keep_mask)


def solution(mesh):
    return jax.shard_map(
        functools.partial(shards, mesh.shape["ep"], mesh.shape["tp"]),
        mesh=mesh,
        in_specs=(
            P("ep", None),
            P("ep", None),
            P(),
            P("ep", None, "tp"),
            P("ep", None, "tp"),
            P("ep", "tp", None),
            P("ep", None),
        ),
        out_specs=P("ep", None),
        check_vma=False,
    )
```

profile of v0, /device:TPU:0, one launch (start us, length us, event | category | flops | bytes accessed | tf_op | source)
XLA Modules:
  0.0 106.4 jit_solution(5848736834375892069)
XLA Ops:
  0.0 0.0 copy-start.1
  0.0 0.0 copy-start
  0.0 2.0 %fusion.10 = f32[128,4]{0,1:T(4,128)S(1)} fusion(bf16[128,6144]{1,0:T(8,128)(2,1)} %param.7, bf16[6144,4]{0,1:T(4,128)(2,1)} %param.9), kind=kOutput, calls=%fused_computation.30 | convolution fusion | flops 6291456 | bytes 1624064 | tf_op jit(solution)/shard_map/dot_general | solution.py:230
  2.0 0.0 copy-done.1
  2.1 0.1 fusion.5
  2.3 0.1 reduce-precision_convert_fusion
  2.4 0.7 pad_maximum_fusion.comb_ref
  3.1 0.0 copy-done
  3.1 3.5 %convolution_convert_fusion = bf16[384,6144]{1,0:T(8,128)(2,1)} fusion(bf16[128,6144]{1,0:T(8,128)(2,1)S(1)} %copy-done, s32[128]{0:T(128)S(1)} %get-tuple-element.17, s32[128]{0:T(128)S(1)} %get-tuple-element.18), kind=kOutput, calls=%fused_computation | convolution fusion | flops 606486528 | bytes 6292480 | tf_op jit(solution)/shard_map/dot_general | solution.py:245
  6.6 97.1 %shard_map.73 = bf16[128,6144]{1,0:T(8,128)(2,1)} custom-call(bf16[4,96,6144]{2,1,0:T(8,128)(2,1)} %bitcast.22, bf16[256,384]{1,0:T(8,128)(2,1)} %pad_maximum_fusion.comb_ref, bf16[6144,1024]{1,0:T(8,128)(2,1)} %bitcast.23, bf16[6144,1024]{1,0:T(8,128)(2,1)} %bitcast.24, bf16[1024,6144]{1,0:T(8,128)(2,1)} %bitcast.25, s32[128,6144]{1,0:T(8,128)} %mask_hbm.1), custom_call_target="tpu_custom_call" | custom-call | tf_op jit(solution)/shard_map/pallas_call | solution.py:257
  103.8 2.7 %copy.12 = bf16[128,6144]{1,0:T(8,128)(2,1)} copy(bf16[128,6144]{1,0:T(8,128)(2,1)} %shard_map.73) | data formatting | bytes 3145728
  (5 shorter events, 0.1 us)
Async XLA Ops:
  0.0 2.0 %copy-start.1 = (s32[128,2]{0,1:T(2,128)S(1)}, s32[128,2]{0,1:T(2,128)}, u32[]{:S(2)}) copy-start(s32[128,2]{0,1:T(2,128)} %param.8) | copy-start | bytes 3076
  0.0 3.1 %copy-start = (bf16[128,6144]{1,0:T(8,128)(2,1)S(1)}, bf16[128,6144]{1,0:T(8,128)(2,1)}, u32[]{:S(2)}) copy-start(bf16[128,6144]{1,0:T(8,128)(2,1)} %param.7) | copy-start | bytes 4718596
where the time goes:
time: 107 us; the launch traced here: 106 us
  Pallas kernels  97.1 us (91%)
  matrix products  5.65 us (5%)
  local copies, waits for them, and re-layouts  2.7 us (3%)
    pallas_call x1, Pallas kernels, shards(): pl.pallas_call(functools.partial(kernel, n_ep, nz), out_shape=jax.ShapeDt...  97.1 us
    dot_general x1, matrix products, shards(): jnp.dot(picker, tokens, preferred_element_type=jnp.float32)  3.49 us
    unnamed x5, local copies, waits for them, and re-layouts  2.7 us

commit v1 on v0

--- a/solution.py
+++ b/solution.py
@@ -21,8 +21,8 @@
 def kernel(
     n_ep, nz, slots_ref, comb_ref, gate_hbm, up_hbm, down_hbm, mask_hbm, out_ref,
     w_gate, w_up, w_down, mask, rows, hidden, pair_out, pair_in, mine, ep_out, ep_in,
-    z_out, z_in, local_sem, disp_s, disp_r, fwd_s, fwd_r, pair_s, pair_r, ep_s, ep_r,
-    z_s, z_r, gat_s, gat_r, gfw_s, gfw_r,
+    z_out, z_in, acc, local_sem, mask_sem, disp_s, disp_r, fwd_s, fwd_r, pair_s, pair_r, ep_s, ep_r,
+    z_s, z_r, b_s, b_r, gfw_s, gfw_r,
 ):
     ep, tp = lax.axis_index("ep"), lax.axis_index("tp")
     z, core = tp // 2, tp % 2
@@ -30,24 +30,22 @@
     cap, width = rows.shape[1], rows.shape[2]
     toks = out_ref.shape[0]
     ff = w_gate.shape[1]
-    half, piece = width // 2, width // (2 * nz)
-    total_rows = n_ep * cap
-
-    rounds = pair_in.shape[0] // nz
-    sub = piece // rounds
-
-    def cols(owner_core, owner_z, turn=None):
-        if turn is None:
-            return pl.ds(pl.multiple_of((owner_core * nz + owner_z) * piece, 128), piece)
-        return pl.ds(pl.multiple_of((owner_core * nz + owner_z) * piece + turn * sub, 128), sub)
-
-    my_half = pl.ds(pl.multiple_of(core * half, 128), half)
+    half = width // 2
+    steps, sub = pair_in.shape[0], pair_in.shape[2]
+
+    def cols(owner_core, s):
+        return pl.ds(pl.multiple_of(owner_core * half + s * sub, 128), sub)
+
+    def root_of(s):
+        return max(0, nz // 2 - 1) + (s % 2 if nz > 1 else 0)
 
     load_own = pltpu.make_async_copy(slots_ref.at[ep], rows.at[0], local_sem.at[0])
     load_gate = pltpu.make_async_copy(gate_hbm, w_gate, local_sem.at[1])
     load_up = pltpu.make_async_copy(up_hbm, w_up, local_sem.at[2])
     load_down = pltpu.make_async_copy(down_hbm, w_down, local_sem.at[3])
-    load_mask = pltpu.make_async_copy(mask_hbm.at[:, cols(core, z)], mask, local_sem.at[4])
+    odd_root = jnp.clip(z - root_of(0), 0, 1)
+    load_mask = [pltpu.make_async_copy(mask_hbm.at[:, cols(core, 2 * j + odd_root)], mask.at[j], mask_sem.at[j])
+                 for j in range(mask.shape[0])]
     for load in (load_own, load_gate, load_up):
         load.start()
 
@@ -104,7 +102,8 @@
     for o in range(1, n_ep):
         send_rows(o, 1, common)
     load_down.start()
-    load_mask.start()
+    for load in load_mask:
+        load.start()
     for o in share_order:
         pass_on(o, 0, shared)
 
@@ -137,6 +136,12 @@
         lax.fori_loop(0, ff // tile, up_step, 0)
 
     load_down.wait()
+    for load in load_mask:
+        load.wait()
+
+    ep_lag, z_lag = 3, 2
+    depth = max(root_of(0), nz - 1 - root_of(0), root_of(1), nz - 1 - root_of(1))
+    pair, exchange = [], [[] for _ in range(steps)]
 
     def pair_sum(s):
         pair[s].wait_recv()
@@ -150,10 +155,90 @@
             exchange[s].append(copy)
             started.append(copy)
 
-    pair, exchange = [], [[] for _ in range(rounds * nz)]
-    for s in range(rounds * nz):
-        turn, owner = s // nz, (z + 1 + s % nz) % nz
-        pair_out[s] = jnp.dot(hidden[...], w_down[:, cols(1 - core, owner, turn)],
+    def inward(s, root):
+        side = jnp.where(z < root, 0, 1)
+        to = jnp.where(z < root, z + 1, z - 1)
+        return remote(z_out.at[s], z_in.at[s, side], z_s.at[s], z_r.at[s, side], (ep, to * 2 + core))
+
+    def from_side(s, side):
+        return remote(z_out.at[s], z_in.at[s, side], z_s.at[s], z_r.at[s, side], partner)
+
+    def outward(s, side):
+        here = out_ref.at[:, cols(core, s)]
+        return remote(here, here, b_s.at[s, side], b_r.at[s], (ep, (z - 1 + 2 * side) * 2 + core))
+
+    def to_partner(s):
+        here = out_ref.at[:, cols(core, s)]
+        return remote(here, here, gfw_s.at[s], gfw_r.at[s], partner)
+
+    def combine(s):
+        for copy in exchange[s]:
+            copy.wait_recv()
+        both = jnp.dot(comb_ref[...], ep_in[s], preferred_element_type=jnp.float32)
+        acc[s % acc.shape[0]] = both[0:toks] + both[toks:]
+
+    def chain(s, k):
+        root = root_of(s)
+        top = max(root, nz - 1 - root)
+        held = s % acc.shape[0]
+        if k < top:
+
+            @pl.when(((z < root) & (z == k)) | ((z > root) & (nz - 1 - z == k)))
+            def _():
+                total = acc[held]
+                if k > 0:
+                    side = jnp.where(z < root, 0, 1)
+                    from_side(s, side).wait_recv()
+                    total = total + z_in[s, side].astype(jnp.float32)
+                z_out[s] = total.astype(jnp.bfloat16)
+                inward(s, root).start()
+
+        elif k == top:
+
+            @pl.when(z == root)
+            def _():
+                total = acc[held]
+                for side in range(2):
+                    if (root > 0, root < nz - 1)[side]:
+                        from_side(s, side).wait_recv()
+                        total = total + z_in[s, side].astype(jnp.float32)
+                keep = mask[s // 2].astype(jnp.float32)
+                out_ref[:, cols(core, s)] = (total * keep * 1.25).astype(jnp.bfloat16)
+                if root > 0:
+                    outward(s, 0).start()
+                if root < nz - 1:
+                    outward(s, 1).start()
+                to_partner(s).start()
+
+        else:
+            away = k - top
+
+            @pl.when((z == root - away) | (z == root + away))
+            def _():
+                outward(s, 0).wait_recv()
+
+                @pl.when((z < root) & (z > 0))
+                def _():
+                    outward(s, 0).start()
+
+                @pl.when((z > root) & (z < nz - 1))
+                def _():
+                    outward(s, 1).start()
+
+                to_partner(s).start()
+
+    def advance(i):
+        for k in range(2 * depth, 0, -1):
+            s = i - ep_lag - k * z_lag
+            if 0 <= s < steps and k <= 2 * max(root_of(s), nz - 1 - root_of(s)):
+                chain(s, k)
+        s = i - ep_lag
+        if 0 <= s < steps:
+            combine(s)
+            chain(s, 0)
+
+    for s in range(steps):
+        pair_out[s] = jnp.dot(hidden[...], w_down[:, cols(1 - core, s)],
                               preferred_element_type=jnp.float32).astype(jnp.bfloat16)
         copy = remote(pair_out.at[s], pair_in.at[s], pair_s.at[s], pair_r.at[s], partner)
         copy.start()
@@ -161,61 +246,33 @@
         started.append(copy)
         if s > 0:
             pair_sum(s - 1)
-        mine[s % 2] = jnp.dot(hidden[...], w_down[:, cols(core, owner, turn)],
+        mine[s % 2] = jnp.dot(hidden[...], w_down[:, cols(core, s)],
                               preferred_element_type=jnp.float32).astype(jnp.bfloat16)
-    pair_sum(rounds * nz - 1)
-
-    load_mask.wait()
-    gather = {}
-    passed = []
-
-    def hand_over(turn):
-        for s in range(1, nz):
-            gather[turn, s].wait_recv()
-            there = out_ref.at[:, cols(core, (z + nz - s) % nz, turn)]
-            copy = remote(there, there, gfw_s.at[turn, s], gfw_r.at[turn, s], partner)
-            copy.start()
-            passed.append(copy)
-            started.append(copy)
-
-    for turn in range(rounds):
-        reduce = []
-        for s in range(nz):
-            step = turn * nz + s
-            owner = (z + 1 + s) % nz
-            for copy in exchange[step]:
-                copy.wait_recv()
-            both = jnp.dot(comb_ref[...], ep_in[step], preferred_element_type=jnp.float32)
-            token_sum = both[0:toks] + both[toks:]
-            if s < nz - 1:
-                z_out[turn, s] = token_sum.astype(jnp.bfloat16)
-                copy = remote(z_out.at[turn, s], z_in.at[turn, s], z_s.at[turn, s], z_r.at[turn, s],
-                              (ep, owner * 2 + core))
-                copy.start()
-                reduce.append(copy)
-                started.append(copy)
-        for s in range(nz - 1):
-            reduce[s].wait_recv()
-            token_sum = token_sum + z_in[turn, s].astype(jnp.float32)
-        keep = mask[:, turn * sub:(turn + 1) * sub].astype(jnp.float32)
-        out_ref[:, cols(core, z, turn)] = (token_sum * keep * 1.25).astype(jnp.bfloat16)
-        here = out_ref.at[:, cols(core, z, turn)]
-        for s in range(1, nz):
-            copy = remote(here, here, gat_s.at[turn, s], gat_r.at[turn, s], (ep, ((z + s) % nz) * 2 + core))
-            copy.start()
-            gather[turn, s] = copy
-            started.append(copy)
-        copy = remote(here, here, gfw_s.at[turn, 0], gfw_r.at[turn, 0], partner)
-        copy.start()
-        passed.append(copy)
-        started.append(copy)
-        if turn > 0:
-            hand_over(turn - 1)
-    hand_over(rounds - 1)
-    for copy in passed:
-        copy.wait_recv()
+        advance(s)
+    pair_sum(steps - 1)
+
+    for i in range(steps, steps + ep_lag + 2 * depth * z_lag + 1):
+        advance(i)
+    for s in range(steps):
+        to_partner(s).wait_recv()
     for copy in started:
         copy.wait_send()
+    for s in range(steps):
+        root = root_of(s)
+
+        @pl.when(z != root)
+        def _():
+            inward(s, root).wait_send()
+
+        @pl.when((z <= root) & (z > 0))
+        def _():
+            outward(s, 0).wait_send()
+
+        @pl.when((z >= root) & (z < nz - 1))
+        def _():
+            outward(s, 1).wait_send()
+
+        to_partner(s).wait_send()
 
 
 def shards(n_ep, n_tp, tokens, expert_ids, router, gate_weight, up_weight, down_weight, keep_mask):
@@ -223,10 +280,9 @@
     toks, width = tokens.shape
     cap = 3 * toks // experts
     nz = n_tp // 2
-    piece = width // n_tp
     total = experts * cap
-    rounds = 3 if piece % 384 == 0 and piece > 384 else 1
-    sub, steps = piece // rounds, rounds * nz
+    sub = 256
+    steps = width // 2 // sub
     logits = jnp.dot(tokens, router, preferred_element_type=jnp.float32)
     numbers = jnp.arange(experts, dtype=jnp.int32)
     onehot3 = expert_ids[:, :, None] == numbers[None, None, :]
@@ -261,17 +317,19 @@
         out_specs=vmem,
         scratch_shapes=[
             pltpu.VMEM((width, ff), bf), pltpu.VMEM((width, ff), bf), pltpu.VMEM((ff, width), bf),
-            pltpu.VMEM((toks, piece), jnp.int32),
+            pltpu.VMEM((steps // 2, toks, sub), jnp.int32),
             pltpu.VMEM((experts, cap, width), bf),
             pltpu.VMEM((total, ff), bf),
             pltpu.VMEM((steps, total, sub), bf), pltpu.VMEM((steps, total, sub), bf),
             pltpu.VMEM((2, total, sub), bf),
             pltpu.VMEM((steps, total - cap, sub), bf), pltpu.VMEM((steps, total, sub), bf),
-            pltpu.VMEM((rounds, nz - 1, toks, sub), bf), pltpu.VMEM((rounds, nz - 1, toks, sub), bf),
-            dma((5,)), dma((3, n_ep)), dma((3, n_ep)), dma((3, n_ep)), dma((3, n_ep)),
+            pltpu.VMEM((steps, toks, sub), bf), pltpu.VMEM((steps, 2, toks, sub), bf),
+            pltpu.VMEM((8, toks, sub), jnp.float32),
+            dma((4,)), dma((steps // 2,)),
+            dma((3, n_ep)), dma((3, n_ep)), dma((3, n_ep)), dma((3, n_ep)),
             dma((steps,)), dma((steps,)), dma((steps, n_ep)), dma((steps, n_ep)),
-            dma((rounds, nz)), dma((rounds, nz)), dma((rounds, nz)), dma((rounds, nz)),
-            dma((rounds, nz)), dma((rounds, nz)),
+            dma((steps,)), dma((steps, 2)), dma((steps, 2)), dma((steps,)),
+            dma((steps,)), dma((steps,)),
         ],
         compiler_params=pltpu.CompilerParams(
             collective_id=0, has_side_effects=True, vmem_limit_bytes=67043328),

time: 107 us -> 97.2 us (0.908)
  Pallas kernels: 97.1 us -> 87.7 us
    pallas_call x1, Pallas kernels: 97.1 us -> 87.7 us  [shards(): pl.pallas_call(functools.partial(kernel, n_ep, nz), out_shape=jax.ShapeDt...]
where the time goes in v1:
time: 97.2 us; the launch traced here: 97 us
  Pallas kernels  87.7 us (90%)
  matrix products  5.66 us (6%)
  local copies, waits for them, and re-layouts  2.7 us (3%)
    pallas_call x1, Pallas kernels, shards(): pl.pallas_call(functools.partial(kernel, n_ep, nz), out_shape=jax.ShapeDt...  87.7 us
    dot_general x1, matrix products, shards(): jnp.dot(picker, tokens, preferred_element_type=jnp.float32)  3.49 us
    unnamed x5, local copies, waits for them, and re-layouts  2.7 us
    dot_general x1, matrix products, shards(): logits = jnp.dot(tokens, router, preferred_element_type=jnp.float32)  2.03 us

profile of v1, /device:TPU:0, one launch (start us, length us, event | category | flops | bytes accessed | tf_op | source)
XLA Modules:
  0.0 97.0 jit_solution(4393482172340827029)
XLA Ops:
  0.0 0.0 copy-start.1
  0.0 0.0 copy-start
  0.0 2.0 %fusion.10 = f32[128,4]{0,1:T(4,128)S(1)} fusion(bf16[128,6144]{1,0:T(8,128)(2,1)} %param.7, bf16[6144,4]{0,1:T(4,128)(2,1)} %param.9), kind=kOutput, calls=%fused_computation.30 | convolution fusion | flops 6291456 | bytes 1624064 | tf_op jit(solution)/shard_map/dot_general | solution.py:286
  2.0 0.0 copy-done.1
  2.1 0.1 fusion.5
  2.3 0.1 reduce-precision_convert_fusion
  2.4 0.7 pad_maximum_fusion.comb_ref
  3.1 0.0 copy-done
  3.1 3.5 %convolution_convert_fusion = bf16[384,6144]{1,0:T(8,128)(2,1)} fusion(bf16[128,6144]{1,0:T(8,128)(2,1)S(1)} %copy-done, s32[128]{0:T(128)S(1)} %get-tuple-element.17, s32[128]{0:T(128)S(1)} %get-tuple-element.18), kind=kOutput, calls=%fused_computation | convolution fusion | flops 606486528 | bytes 6292480 | tf_op jit(solution)/shard_map/dot_general | solution.py:301
  6.6 87.7 %shard_map.73 = bf16[128,6144]{1,0:T(8,128)(2,1)} custom-call(bf16[4,96,6144]{2,1,0:T(8,128)(2,1)} %bitcast.22, bf16[256,384]{1,0:T(8,128)(2,1)} %pad_maximum_fusion.comb_ref, bf16[6144,1024]{1,0:T(8,128)(2,1)} %bitcast.23, bf16[6144,1024]{1,0:T(8,128)(2,1)} %bitcast.24, bf16[1024,6144]{1,0:T(8,128)(2,1)} %bitcast.25, s32[128,6144]{1,0:T(8,128)} %mask_hbm.1), custom_call_target="tpu_custom_call" | custom-call | tf_op jit(solution)/shard_map/pallas_call | solution.py:313
  94.3 2.7 %copy.12 = bf16[128,6144]{1,0:T(8,128)(2,1)} copy(bf16[128,6144]{1,0:T(8,128)(2,1)} %shard_map.73) | data formatting | bytes 3145728
  (5 shorter events, 0.1 us)
Async XLA Ops:
  0.0 2.0 %copy-start.1 = (s32[128,2]{0,1:T(2,128)S(1)}, s32[128,2]{0,1:T(2,128)}, u32[]{:S(2)}) copy-start(s32[128,2]{0,1:T(2,128)} %param.8) | copy-start | bytes 3076
  0.0 3.1 %copy-start = (bf16[128,6144]{1,0:T(8,128)(2,1)S(1)}, bf16[128,6144]{1,0:T(8,128)(2,1)}, u32[]{:S(2)}) copy-start(bf16[128,6144]{1,0:T(8,128)(2,1)} %param.7) | copy-start | bytes 4718596

commit v2 on v1

v2 whole, which is shorter than its diff:
```python
import functools

import jax
import jax.numpy as jnp
from jax import lax
from jax.experimental import pallas as pl
from jax.experimental.pallas import tpu as pltpu
from jax.sharding import PartitionSpec as P

MESH = pl.DeviceIdType.MESH


def flip(index, offset, count):
    out, bit = 0, 1
    while bit < count:
        out = out + ((index // bit + offset // bit) % 2) * bit
        bit *= 2
    return out


def kernel(
    n_ep, nz, ids_ref, router_ref, tokens_hbm, gate_hbm, up_hbm, down_hbm, mask_hbm, out_ref,
    tokens, w_gate, w_up, w_down, mask, rows, gate_up, hidden, comb, pair_out, pair_in, mine, ep_out, ep_in,
    z_out, z_in, acc, local_sem, w_sem, disp_s, disp_r, share_s, share_r, fwd_s, fwd_r,
    pair_s, pair_r, ep_s, ep_r, z_s, z_r, b_s, b_r, gfw_s, gfw_r,
):
    ep, tp = lax.axis_index("ep"), lax.axis_index("tp")
    z, core = tp // 2, tp % 2
    partner = (ep, z * 2 + (1 - core))
    cap, width = rows.shape[1], rows.shape[2]
    toks = out_ref.shape[0]
    ff = w_gate.shape[1]
    half = width // 2
    steps, sub = pair_in.shape[0], pair_in.shape[2]
    groups = fwd_r.shape[0]
    experts = router_ref.shape[0]
    wide = half // groups
    total_rows = n_ep * cap

    def cols(owner_core, s):
        return pl.ds(pl.multiple_of(owner_core * half + s * sub, 128), sub)

    def root_of(s):
        return max(0, nz // 2 - 1) + (s % 2 if nz > 1 else 0)

    load_tokens = pltpu.make_async_copy(tokens_hbm, tokens, local_sem.at[0])
    load_tokens.start()

    def load_weights(g):
        for h in range(2):
            at = pl.ds(h * half + g * wide, wide)
            for src, dst in ((gate_hbm, w_gate), (up_hbm, w_up)):
                pltpu.make_async_copy(src.at[at], dst.at[at], w_sem.at[g]).start()

    def wait_weights(g):
        at = pl.ds(0, 4 * wide)
        pltpu.make_async_copy(gate_hbm.at[at], w_gate.at[at], w_sem.at[g]).wait()

    load_down = pltpu.make_async_copy(down_hbm, w_down, local_sem.at[1])
    odd_root = jnp.clip(z - root_of(0), 0, 1)
    load_mask = [pltpu.make_async_copy(mask_hbm.at[:, cols(core, 2 * j + odd_root)],
                                       mask.at[:, j * sub:(j + 1) * sub], local_sem.at[2])
                 for j in range(steps // 2)]

    barrier = pltpu.get_barrier_semaphore()
    for peer in [(flip(ep, o, n_ep), tp) for o in range(1, n_ep)] + [partner]:
        pl.semaphore_signal(barrier, inc=1, device_id=peer, device_id_type=MESH)

    @pl.when(z > 0)
    def _():
        pl.semaphore_signal(barrier, inc=1, device_id=(ep, (z - 1) * 2 + core), device_id_type=MESH)

    @pl.when(z < nz - 1)
    def _():
        pl.semaphore_signal(barrier, inc=1, device_id=(ep, (z + 1) * 2 + core), device_id_type=MESH)

    def remote(src, dst, send, recv, device):
        return pltpu.make_async_remote_copy(
            src_ref=src, dst_ref=dst, send_sem=send, recv_sem=recv,
            device_id=device, device_id_type=MESH,
        )

    odd = z % 2
    z_pair = (ep, (z + 1 - 2 * odd) * 2 + core)

    first_id, second_id = ids_ref[0:1, :], ids_ref[1:2, :]
    numbers = lax.broadcasted_iota(jnp.int32, (experts, toks), 0)
    is_first, is_second = numbers == first_id, numbers == second_id
    named = jnp.where(is_first, 1.0, 0.0) + jnp.where(is_second, 1.0, 0.0)
    before = (lax.broadcasted_iota(jnp.int32, (toks, toks), 0) < lax.broadcasted_iota(jnp.int32, (toks, toks), 1))
    ranks = jnp.dot(named.astype(jnp.bfloat16), jnp.where(before, 1.0, 0.0).astype(jnp.bfloat16),
                    preferred_element_type=jnp.float32)

    def of_choice(chosen, values):
        return jnp.sum(jnp.where(chosen, values, 0.0), axis=0, keepdims=True)

    slots = of_choice(is_first, ranks), of_choice(is_second, ranks)
    places = [(number * cap).astype(jnp.float32) + slot for number, slot in zip((first_id, second_id), slots)]

    def picker(owner):
        lines = (lax.broadcasted_iota(jnp.int32, (cap, toks), 0) + owner * cap).astype(jnp.float32)
        return jnp.where((places[0] == lines) | (places[1] == lines), 1.0, 0.0).astype(jnp.bfloat16)

    def piece_of(kind, g):
        return 3 * g + (2 * odd, 1, 2 - 2 * odd)[kind]

    def dispatch(kind, g, o):
        s = piece_of(kind, g)
        return remote(ep_out.at[s, pl.ds((o - 1) * cap, cap), :], rows.at[o, :, cols(core, s)],
                      disp_s.at[0], disp_r.at[kind, g], (flip(ep, o, n_ep), tp))

    def guests(kind, g):
        return rows.at[pl.ds(1, n_ep - 1), :, cols(core, piece_of(kind, g))]

    def share(g):
        return remote(guests(0, g), guests(0, g), share_s.at[0], share_r.at[g], z_pair)

    def forward(kind, g):
        return remote(guests(kind, g), guests(kind, g), fwd_s.at[0], fwd_r.at[g], partner)

    def pass_on(kind, g):
        if kind < 2:
            remote(guests(kind, g), guests(kind, g), disp_s.at[0], disp_r.at[kind, g], partner).wait_recv()
        else:
            share(g).wait_recv()
        if kind == 0:
            share(g).start()
        forward(kind, g).start()

    order = [(0, 0)]
    for g in range(groups):
        if g + 1 < groups:
            order.append((0, g + 1))
        order.append((1, g))
    with jax.named_scope("tokens"):
        load_tokens.wait()
    for g in range(groups):
        load_weights(g)
    others = jnp.concatenate([picker(flip(ep, o, n_ep)) for o in range(1, n_ep)], axis=0)
    for n, (kind, g) in enumerate(order):
        s = piece_of(kind, g)
        ep_out[s] = jnp.dot(others, tokens[:, cols(core, s)],
                            preferred_element_type=jnp.float32).astype(jnp.bfloat16)
        if n == 0:
            peers = n_ep + jnp.where(z > 0, 1, 0) + jnp.where(z < nz - 1, 1, 0)
            with jax.named_scope("barrier"):
                pl.semaphore_wait(barrier, peers)
        for o in [n_ep - 1] + list(range(1, n_ep - 1)):
            dispatch(kind, g, o).start()
    load_down.start()
    for load in load_mask:
        load.start()

    own = picker(ep)
    strip = width // 6
    for n in range(6):
        rows[0, :, n * strip:(n + 1) * strip] = jnp.dot(
            own, tokens[:, n * strip:(n + 1) * strip], preferred_element_type=jnp.float32).astype(jnp.bfloat16)

    logits = lax.dot_general(router_ref[...], tokens[...], (((1,), (1,)), ((), ())),
                             preferred_element_type=jnp.float32)
    ahead = of_choice(is_first, logits) - of_choice(is_second, logits)
    lines = lax.broadcasted_iota(jnp.int32, (total_rows, toks), 0).astype(jnp.float32)
    turned = [(jnp.bitwise_xor(number, ep) * cap).astype(jnp.float32) + slot
              for number, slot in zip((first_id, second_id), slots)]
    mixed = (jnp.where(turned[0] == lines, jax.nn.sigmoid(ahead), 0.0)
             + jnp.where(turned[1] == lines, jax.nn.sigmoid(-ahead), 0.0))
    comb[...] = mixed.T.astype(jnp.bfloat16)

    tile = min(256, ff)
    tiles = ff // tile

    def up_tile(g, n):
        at = slice(n * tile, (n + 1) * tile)
        sums = []
        for i, w in enumerate((w_gate, w_up)):
            part = None
            for h in range(2):
                k = slice(h * half + g * wide, h * half + (g + 1) * wide)
                dot = jnp.dot(rows[:, :, k].reshape(total_rows, wide), w[k, at],
                              preferred_element_type=jnp.float32)
                part = dot if part is None else part + dot
            if g > 0:
                part = part + gate_up[i, :, at]
            if g < groups - 1:
                gate_up[i, :, at] = part
            sums.append(part)
        if g == groups - 1:
            hidden[:, at] = (jax.nn.silu(sums[0]) * sums[1]).astype(jnp.bfloat16)

    todo = []
    for g in range(groups):
        todo += [(0, g), (1, g - 1), (2, g - 1)] if g else [(0, 0)]
    todo += [(1, groups - 1), (2, groups - 1)]
    for g in range(groups):
        with jax.named_scope(f"pass_{g}"):
            while any((kind, g) in todo for kind in range(3)):
                pass_on(*todo.pop(0))
        with jax.named_scope(f"arrive_{g}"):
            wait_weights(g)
            here = rows.at[pl.ds(1, n_ep - 1), :, pl.ds(0, wide)]
            remote(here, here, fwd_s.at[0], fwd_r.at[g], partner).wait_recv()
        with jax.named_scope(f"up_{g}"):
            for n in range(tiles):
                up_tile(g, n)
                if n == tiles // 2 - 1 and todo:
                    pass_on(*todo.pop(0))

    load_down.wait()
    pltpu.make_async_copy(mask_hbm.at[:, 0:mask.shape[1]], mask, local_sem.at[2]).wait()
    staged = ep_out.at[pl.ds(0, len(order))]
    remote(staged, staged, disp_s.at[0], disp_r.at[0, 0], partner).wait_send()

    ep_lag, z_lag = 3, 2
    depth = max(root_of(0), nz - 1 - root_of(0), root_of(1), nz - 1 - root_of(1))
    pair = []

    def pair_sum(s):
        pair[s].wait_recv()
        summed = (mine[s % 2].astype(jnp.float32) + pair_in[s].astype(jnp.float32)).astype(jnp.bfloat16)
        ep_in[s, 0:cap, :] = summed[0:cap]
        ep_out[s] = summed[cap:]
        for o in range(1, n_ep):
            copy = remote(ep_out.at[s, pl.ds((o - 1) * cap, cap), :], ep_in.at[s, pl.ds(o * cap, cap), :],
                          ep_s.at[0], ep_r.at[s], (flip(ep, o, n_ep), tp))
            copy.start()

    def inward(s, root):
        side = jnp.where(z < root, 0, 1)
        to = jnp.where(z < root, z + 1, z - 1)
        return remote(z_out.at[s], z_in.at[s, side], z_s.at[s % 2], z_r.at[s, side], (ep, to * 2 + core))

    def from_side(s, side):
        return remote(z_out.at[s], z_in.at[s, side], z_s.at[s % 2], z_r.at[s, side], partner)

    def outward(s, side):
        here = out_ref.at[:, cols(core, s)]
        return remote(here, here, b_s.at[s % 2, side], b_r.at[s], (ep, (z - 1 + 2 * side) * 2 + core))

    def to_partner(s):
        here = out_ref.at[:, cols(core, s)]
        return remote(here, here, gfw_s.at[0], gfw_r.at[0], partner)

    def combine(s):
        arrived = ep_in.at[s, pl.ds(cap, total_rows - cap), :]
        remote(arrived, arrived, ep_s.at[0], ep_r.at[s], partner).wait_recv()
        acc[s % acc.shape[0]] = jnp.dot(comb[...], ep_in[s], preferred_element_type=jnp.float32)

    def chain(s, k):
        root = root_of(s)
        top = max(root, nz - 1 - root)
        held = s % acc.shape[0]
        if k < top:

            @pl.when(((z < root) & (z == k)) | ((z > root) & (nz - 1 - z == k)))
            def _():
                total = acc[held]
                if k > 0:
                    side = jnp.where(z < root, 0, 1)
                    from_side(s, side).wait_recv()
                    total = total + z_in[s, side].astype(jnp.float32)
                z_out[s] = total.astype(jnp.bfloat16)
                inward(s, root).start()

        elif k == top:

            @pl.when(z == root)
            def _():
                total = acc[held]
                for side in range(2):
                    if (root > 0, root < nz - 1)[side]:
                        from_side(s, side).wait_recv()
                        total = total + z_in[s, side].astype(jnp.float32)
                keep = mask[:, (s // 2) * sub:(s // 2 + 1) * sub].astype(jnp.float32)
                out_ref[:, cols(core, s)] = (total * keep * 1.25).astype(jnp.bfloat16)
                if root > 0:
                    outward(s, 0).start()
                if root < nz - 1:
                    outward(s, 1).start()
                to_partner(s).start()

        else:
            away = k - top

            @pl.when((z == root - away) | (z == root + away))
            def _():
                outward(s, 0).wait_recv()

                @pl.when((z < root) & (z > 0))
                def _():
                    outward(s, 0).start()

                @pl.when((z > root) & (z < nz - 1))
                def _():
                    outward(s, 1).start()

                to_partner(s).start()

    def advance(i):
        for k in range(2 * depth, 0, -1):
            s = i - ep_lag - k * z_lag
            if 0 <= s < steps and k <= 2 * max(root_of(s), nz - 1 - root_of(s)):
                chain(s, k)
        s = i - ep_lag
        if 0 <= s < steps:
            combine(s)
            chain(s, 0)

    for s in range(steps):
        pair_out[s] = jnp.dot(hidden[...], w_down[:, cols(1 - core, s)],
                              preferred_element_type=jnp.float32).astype(jnp.bfloat16)
        copy = remote(pair_out.at[s], pair_in.at[s], pair_s.at[0], pair_r.at[s], partner)
        copy.start()
        pair.append(copy)
        if s > 0:
            pair_sum(s - 1)
        mine[s % 2] = jnp.dot(hidden[...], w_down[:, cols(core, s)],
                              preferred_element_type=jnp.float32).astype(jnp.bfloat16)
        advance(s)
    pair_sum(steps - 1)

    for i in range(steps, steps + ep_lag + 2 * depth * z_lag + 1):
        advance(i)
    mine_half = out_ref.at[:, pl.ds(0, half)]
    handed = remote(mine_half, mine_half, gfw_s.at[0], gfw_r.at[0], partner)
    with jax.named_scope("partner_recv"):
        handed.wait_recv()
    with jax.named_scope("sends"):
        handed.wait_send()
        remote(ep_out, ep_out, ep_s.at[0], ep_r.at[0], partner).wait_send()
        remote(pair_out, pair_out, pair_s.at[0], pair_r.at[0], partner).wait_send()
        shared = rows.at[pl.ds(1, n_ep - 1), :, pl.ds(0, groups * sub)]
        remote(shared, shared, share_s.at[0], share_r.at[0], partner).wait_send()
        passed = rows.at[pl.ds(1, n_ep - 1), :, pl.ds(0, half)]
        remote(passed, passed, fwd_s.at[0], fwd_r.at[0], partner).wait_send()
        quarter = out_ref.at[:, pl.ds(0, half // 2)]
        for parity in range(2):
            root = root_of(parity)

            @pl.when(z != root)
            def _():
                sums = z_out.at[pl.ds(0, steps // 2)]
                remote(sums, sums, z_s.at[parity], z_r.at[0, 0], partner).wait_send()

            @pl.when((z <= root) & (z > 0))
            def _():
                remote(quarter, quarter, b_s.at[parity, 0], b_r.at[0], partner).wait_send()

            @pl.when((z >= root) & (z < nz - 1))
            def _():
                remote(quarter, quarter, b_s.at[parity, 1], b_r.at[0], partner).wait_send()


def shards(n_ep, n_tp, tokens, expert_ids, router, gate_weight, up_weight, down_weight, keep_mask):
    experts = router.shape[1]
    toks, width = tokens.shape
    cap = 3 * toks // experts
    nz = n_tp // 2
    total = experts * cap
    sub = 256
    steps = width // 2 // sub
    groups = steps // 3
    w_gate, w_up, w_down = gate_weight[0], up_weight[0], down_weight[0]
    ff = w_gate.shape[1]
    vmem, hbm = pl.BlockSpec(memory_space=pltpu.VMEM), pl.BlockSpec(memory_space=pl.ANY)
    bf = jnp.bfloat16
    dma = pltpu.SemaphoreType.DMA
    return pl.pallas_call(
        functools.partial(kernel, n_ep, nz),
        out_shape=jax.ShapeDtypeStruct((toks, width), bf),
        in_specs=[vmem, vmem, hbm, hbm, hbm, hbm, hbm],
        out_specs=vmem,
        scratch_shapes=[
            pltpu.VMEM((toks, width), bf),
            pltpu.VMEM((width, ff), bf), pltpu.VMEM((width, ff), bf), pltpu.VMEM((ff, width), bf),
            pltpu.VMEM((toks, width // 4), jnp.int32),
            pltpu.VMEM((experts, cap, width), bf),
            pltpu.VMEM((2, total, ff), jnp.float32),
            pltpu.VMEM((total, ff), bf),
            pltpu.VMEM((toks, total), bf),
            pltpu.VMEM((steps, total, sub), bf), pltpu.VMEM((steps, total, sub), bf),
            pltpu.VMEM((2, total, sub), bf),
            pltpu.VMEM((steps, total - cap, sub), bf), pltpu.VMEM((steps, total, sub), bf),
            pltpu.VMEM((steps, toks, sub), bf), pltpu.VMEM((steps, 2, toks, sub), bf),
            pltpu.VMEM((8, toks, sub), jnp.float32),
            dma((3,)), dma((groups,)),
            dma((1,)), dma((2, groups)), dma((1,)), dma((groups,)), dma((1,)), dma((groups,)),
            dma((1,)), dma((steps,)), dma((1,)), dma((steps,)),
            dma((2,)), dma((steps, 2)), dma((2, 2)), dma((steps,)),
            dma((1,)), dma((1,)),
        ],
        compiler_params=pltpu.CompilerParams(
            collective_id=0, has_side_effects=True, vmem_limit_bytes=67043328),
    )(expert_ids.T, router.T, tokens, w_gate, w_up, w_down, keep_mask)


def solution(mesh):
    return jax.shard_map(
        functools.partial(shards, mesh.shape["ep"], mesh.shape["tp"]),
        mesh=mesh,
        in_specs=(
            P("ep", None),
            P("ep", None),
            P(),
            P("ep", None, "tp"),
            P("ep", None, "tp"),
            P("ep", "tp", None),
            P("ep", None),
        ),
        out_specs=P("ep", None),
        check_vma=False,
    )
```

time: 97.2 us -> 82.3 us (0.85)
  Pallas kernels: 87.7 us -> 79.4 us
  matrix products: 5.66 us -> 0 us
    pallas_call x1, Pallas kernels: 87.7 us -> 79.4 us  [shards(): pl.pallas_call(functools.partial(kernel, n_ep, nz), out_shape=jax.ShapeDt...]
    dot_general x3 -> x0, matrix products: 5.66 us -> none  [the longest x1 3.49 us: shards(): jnp.dot(picker, tokens, preferred_element_type=jnp.float32)]
    unnamed x5 -> x1, local copies, waits for them, and re-layouts: 2.7 us -> 2.69 us
where the time goes in v2:
time: 82.3 us; the launch traced here: 82.1 us
  Pallas kernels  79.4 us (96%)
  local copies, waits for them, and re-layouts  2.69 us (3%)
    pallas_call x1, Pallas kernels, shards(): pl.pallas_call(functools.partial(kernel, n_ep, nz), out_shape=jax.ShapeDt...  79.4 us
    unnamed x1, local copies, waits for them, and re-layouts  2.69 us

profile of v2, /device:TPU:0, one launch (start us, length us, event | category | flops | bytes accessed | tf_op | source)
XLA Modules:
  0.0 82.1 jit_solution(3415704639176753811)
XLA Ops:
  0.0 79.4 %shard_map.73 = bf16[128,6144]{1,0:T(8,128)(2,1)} custom-call(s32[2,128]{1,0:T(2,128)} %bitcast.9, bf16[4,6144]{1,0:T(4,128)(2,1)} %bitcast.8, bf16[128,6144]{1,0:T(8,128)(2,1)} %tokens_hbm.1, bf16[6144,1024]{1,0:T(8,128)(2,1)} %bitcast.5, bf16[6144,1024]{1,0:T(8,128)(2,1)} %bitcast.6, bf16[1024,6144]{1,0:T(8,128)(2,1)} %bitcast.7, s32[128,6144]{1,0:T(8,128)} %mask_hbm.1), custom_call_target="tpu_custom_call" | custom-call | tf_op jit(solution)/shard_map/pallas_call | solution.py:368
  79.4 2.7 %copy.9 = bf16[128,6144]{1,0:T(8,128)(2,1)} copy(bf16[128,6144]{1,0:T(8,128)(2,1)} %shard_map.73) | data formatting | bytes 3145728

commit v3 on v2

v3 whole, which is shorter than its diff:
```python
import functools

import jax
import jax.numpy as jnp
from jax import lax
from jax.experimental import pallas as pl
from jax.experimental.pallas import tpu as pltpu
from jax.sharding import PartitionSpec as P

MESH = pl.DeviceIdType.MESH


def flip(index, offset, count):
    out, bit = 0, 1
    while bit < count:
        out = out + ((index // bit + offset // bit) % 2) * bit
        bit *= 2
    return out


def chunk_widths(half, sub):
    return [sub] * (half // sub - 2) + [sub // 2] * 4


def kernel(
    n_ep, nz, ids_ref, router_ref, tokens_hbm, gate_hbm, up_hbm, down_hbm, mask_hbm, out_ref,
    tokens, w_gate, w_up, w_down, mask, rows, gate_up, hidden, comb, pair_out, pair_in, mine, ep_out, ep_in,
    z_out, z_in, far_in, acc, local_sem, w_sem, disp_s, disp_r, share_s, share_r, fwd_s, fwd_r,
    pair_s, pair_r, ep_s, ep_r, z_s, z_r, far_s, far_r, b_s, b_r, gfw_s, gfw_r,
):
    ep, tp = lax.axis_index("ep"), lax.axis_index("tp")
    z, core = tp // 2, tp % 2
    partner = (ep, z * 2 + (1 - core))
    cap, width = rows.shape[1], rows.shape[2]
    toks = out_ref.shape[0]
    ff = w_gate.shape[1]
    half = width // 2
    sub = pair_in.shape[2]
    widths = chunk_widths(half, sub)
    steps, places_of = len(widths), [sum(widths[:n]) for n in range(len(widths))]
    direct = steps - far_in.shape[0]
    groups = fwd_r.shape[1]
    experts = router_ref.shape[0]
    wide = half // groups
    total_rows = n_ep * cap

    def piece(owner_core, s):
        return pl.ds(pl.multiple_of(owner_core * half + s * sub, 128), sub)

    def cols(owner_core, s):
        return pl.ds(pl.multiple_of(owner_core * half + places_of[s], 128), widths[s])

    def own_place(s):
        start = sum(widths[s % 2:s:2])
        return slice(start, start + widths[s])

    def root_of(s):
        return nz // 2 - 1 + (s + core) % 2

    load_tokens = pltpu.make_async_copy(tokens_hbm, tokens, local_sem.at[0])
    load_tokens.start()

    def load_weights(g):
        for h in range(2):
            at = pl.ds(h * half + g * wide, wide)
            for src, dst in ((gate_hbm, w_gate), (up_hbm, w_up)):
                pltpu.make_async_copy(src.at[at], dst.at[at], w_sem.at[g]).start()

    def wait_weights(g):
        at = pl.ds(0, 4 * wide)
        pltpu.make_async_copy(gate_hbm.at[at], w_gate.at[at], w_sem.at[g]).wait()

    load_down = pltpu.make_async_copy(down_hbm, w_down, local_sem.at[1])
    top = nz // 2
    odd_root = (jnp.clip(z - (top - 1), 0, 1) + core) % 2
    load_mask = [pltpu.make_async_copy(mask_hbm.at[:, pl.ds(pl.multiple_of(
        core * half + places_of[2 * j] + odd_root * widths[2 * j], 128), widths[2 * j])],
        mask.at[:, own_place(2 * j)], local_sem.at[2]) for j in range(steps // 2)]

    barrier = pltpu.get_barrier_semaphore()
    peers = [(flip(ep, o, n_ep), tp) for o in range(1, n_ep)] + [partner]
    peers += [(ep, ((z + n) % nz) * 2 + core) for n in range(1, nz)]
    for peer in peers:
        pl.semaphore_signal(barrier, inc=1, device_id=peer, device_id_type=MESH)

    def remote(src, dst, send, recv, device):
        return pltpu.make_async_remote_copy(
            src_ref=src, dst_ref=dst, send_sem=send, recv_sem=recv,
            device_id=device, device_id_type=MESH,
        )

    odd = z % 2
    z_pair = (ep, (z + 1 - 2 * odd) * 2 + core)

    first_id, second_id = ids_ref[0:1, :], ids_ref[1:2, :]
    numbers = lax.broadcasted_iota(jnp.int32, (experts, toks), 0)
    is_first, is_second = numbers == first_id, numbers == second_id
    named = jnp.where(is_first, 1.0, 0.0) + jnp.where(is_second, 1.0, 0.0)
    before = (lax.broadcasted_iota(jnp.int32, (toks, toks), 0) < lax.broadcasted_iota(jnp.int32, (toks, toks), 1))
    ranks = jnp.dot(named.astype(jnp.bfloat16), jnp.where(before, 1.0, 0.0).astype(jnp.bfloat16),
                    preferred_element_type=jnp.float32)

    def of_choice(chosen, values):
        return jnp.sum(jnp.where(chosen, values, 0.0), axis=0, keepdims=True)

    slots = of_choice(is_first, ranks), of_choice(is_second, ranks)
    places = [(number * cap).astype(jnp.float32) + slot for number, slot in zip((first_id, second_id), slots)]

    def picker(owner):
        lines = (lax.broadcasted_iota(jnp.int32, (cap, toks), 0) + owner * cap).astype(jnp.float32)
        return jnp.where((places[0] == lines) | (places[1] == lines), 1.0, 0.0).astype(jnp.bfloat16)

    def piece_of(kind, g):
        return 3 * g + (2 * odd, 1, 2 - 2 * odd)[kind]

    def dispatch(kind, g, o):
        s = piece_of(kind, g)
        return remote(ep_out.at[s, pl.ds((o - 1) * cap, cap), :], rows.at[o, :, piece(core, s)],
                      disp_s.at[0], disp_r.at[kind, g], (flip(ep, o, n_ep), tp))

    def guests(kind, g):
        return rows.at[pl.ds(1, n_ep - 1), :, piece(core, piece_of(kind, g))]

    def share(g):
        return remote(guests(0, g), guests(0, g), share_s.at[0], share_r.at[g], z_pair)

    def forward(kind, g):
        return remote(guests(kind, g), guests(kind, g), fwd_s.at[0], fwd_r.at[kind, g], partner)

    def pass_on(kind, g):
        if kind < 2:
            remote(guests(kind, g), guests(kind, g), disp_s.at[0], disp_r.at[kind, g], partner).wait_recv()
        else:
            share(g).wait_recv()
        if kind == 0:
            share(g).start()
        forward(kind, g).start()

    order = [(0, 0)]
    for g in range(groups):
        if g + 1 < groups:
            order.append((0, g + 1))
        order.append((1, g))
    with jax.named_scope("tokens"):
        load_tokens.wait()
    for g in range(groups):
        load_weights(g)
    others = jnp.concatenate([picker(flip(ep, o, n_ep)) for o in range(1, n_ep)], axis=0)
    for n, (kind, g) in enumerate(order):
        s = piece_of(kind, g)
        ep_out[s] = jnp.dot(others, tokens[:, piece(core, s)],
                            preferred_element_type=jnp.float32).astype(jnp.bfloat16)
        if n == 0:
            with jax.named_scope("barrier"):
                pl.semaphore_wait(barrier, len(peers))
        for o in [n_ep - 1] + list(range(1, n_ep - 1)):
            dispatch(kind, g, o).start()
    load_down.start()
    for load in load_mask:
        load.start()

    own = picker(ep)
    strip = width // 6
    for n in range(6):
        rows[0, :, n * strip:(n + 1) * strip] = jnp.dot(
            own, tokens[:, n * strip:(n + 1) * strip], preferred_element_type=jnp.float32).astype(jnp.bfloat16)

    logits = lax.dot_general(router_ref[...], tokens[...], (((1,), (1,)), ((), ())),
                             preferred_element_type=jnp.float32)
    ahead = of_choice(is_first, logits) - of_choice(is_second, logits)
    lines = lax.broadcasted_iota(jnp.int32, (total_rows, toks), 0).astype(jnp.float32)
    turned = [(jnp.bitwise_xor(number, ep) * cap).astype(jnp.float32) + slot
              for number, slot in zip((first_id, second_id), slots)]
    mixed = (jnp.where(turned[0] == lines, jax.nn.sigmoid(ahead), 0.0)
             + jnp.where(turned[1] == lines, jax.nn.sigmoid(-ahead), 0.0))
    comb[...] = mixed.T.astype(jnp.bfloat16)

    tile = min(256, ff)
    tiles = ff // tile

    def up(pair, lower, upper, first, last):
        for kind, g in pair if lower == 0 else ():
            wait_weights_once(g)
            here = guests(kind, g)
            remote(here, here, fwd_s.at[0], fwd_r.at[kind, g], partner).wait_recv()
        strips = [piece(h, piece_of(kind, g)) for kind, g in pair for h in range(2)]

        def step(n, carry):
            at = pl.ds(pl.multiple_of(n * tile, tile), tile)
            sums = []
            for i, w in enumerate((w_gate, w_up)):
                part = None
                for k in strips:
                    dot = jnp.dot(rows[:, :, k].reshape(total_rows, sub), w[k, at],
                                  preferred_element_type=jnp.float32)
                    part = dot if part is None else part + dot
                if not first:
                    part = part + gate_up[i, :, at]
                if not last:
                    gate_up[i, :, at] = part
                sums.append(part)
            if last:
                hidden[:, at] = (jax.nn.silu(sums[0]) * sums[1]).astype(jnp.bfloat16)
            return carry

        lax.fori_loop(lower, upper, step, 0)

    loaded = set()

    def wait_weights_once(g):
        if g not in loaded:
            loaded.add(g)
            wait_weights(g)

    link, share_link, hop, cross, unit = 2.26, 3.4, 1.8, 1.4, 2.3
    passes, busy = [], 0.0
    for n, (kind, g) in enumerate(order):
        landed = link * (n + 1) + hop
        passes.append((landed, kind, g))
        if kind == 0:
            busy = max(busy, landed) + share_link
            passes.append((busy + hop, 2, g))
    passes.sort()
    due = [(landed, pass_on, (kind, g)) for landed, kind, g in passes]
    clock = 0.0
    for n in range(0, len(passes), 2):
        clock = max(clock, passes[n + 1][0] + cross)
        pair = [given[1:] for given in passes[n:n + 2]]
        for lower, upper in ((0, tiles // 2), (tiles // 2, tiles)):
            due.append((clock, up, (pair, lower, upper, n == 0, n + 2 == len(passes))))
            clock += unit / 2
    for _, action, given in sorted(due, key=lambda event: event[0]):
        with jax.named_scope(action.__name__ + "_".join(str(x) for x in given[:2]).replace(" ", "")):
            action(*given)

    load_down.wait()
    pltpu.make_async_copy(mask_hbm.at[:, 0:mask.shape[1]], mask, local_sem.at[2]).wait()
    staged = ep_out.at[pl.ds(0, len(order))]
    remote(staged, staged, disp_s.at[0], disp_r.at[0, 0], partner).wait_send()

    def within(s):
        return pl.ds(places_of[s] % sub, widths[s])

    def box(s):
        return places_of[s] // sub

    def to_pair(s):
        return remote(pair_out.at[box(s), :, within(s)], pair_in.at[box(s), :, within(s)], pair_s.at[0], pair_r.at[s], partner)

    def down(s):
        pair_out[box(s), :, within(s)] = jnp.dot(hidden[...], w_down[:, cols(1 - core, s)],
                                            preferred_element_type=jnp.float32).astype(jnp.bfloat16)
        mine[s % 2, :, within(s)] = jnp.dot(hidden[...], w_down[:, cols(core, s)],
                                            preferred_element_type=jnp.float32).astype(jnp.bfloat16)
        to_pair(s).start()
        if s > 0:
            pair_sum(s - 1)
        if s == steps - 1:
            pair_sum(s)

    def pair_sum(s):
        at = within(s)
        to_pair(s).wait_recv()
        summed = (mine[s % 2, :, at].astype(jnp.float32) + pair_in[box(s), :, at].astype(jnp.float32)).astype(jnp.bfloat16)
        ep_in[box(s), 0:cap, at] = summed[0:cap]
        ep_out[box(s), :, at] = summed[cap:]
        for o in range(1, n_ep):
            remote(ep_out.at[box(s), pl.ds((o - 1) * cap, cap), at], ep_in.at[box(s), pl.ds(o * cap, cap), at],
                   ep_s.at[0], ep_r.at[s], (flip(ep, o, n_ep), tp)).start()

    def inward(s, root):
        side = jnp.where(z < root, 0, 1)
        to = jnp.where(z < root, z + 1, z - 1)
        return remote(z_out.at[box(s)], z_in.at[s, side], z_s.at[s % 2], z_r.at[s, side], (ep, to * 2 + core))

    def from_side(s, side):
        return remote(z_out.at[box(s)], z_in.at[s, side], z_s.at[s % 2], z_r.at[s, side], partner)

    def outward(s, side):
        here = out_ref.at[:, cols(core, s)]
        return remote(here, here, b_s.at[s % 2, side], b_r.at[s], (ep, (z - 1 + 2 * side) * 2 + core))

    def to_partner(s):
        here = out_ref.at[:, cols(core, s)]
        return remote(here, here, gfw_s.at[0], gfw_r.at[0], partner)

    def finish(s, total):
        keep = mask[:, own_place(s)].astype(jnp.float32)
        out_ref[:, cols(core, s)] = (total * keep * 1.25).astype(jnp.bfloat16)

    def combine(s):
        at = within(s)
        arrived = ep_in.at[box(s), pl.ds(cap, total_rows - cap), at]
        remote(arrived, arrived, ep_s.at[0], ep_r.at[s], partner).wait_recv()
        acc[s % acc.shape[0], :, at] = jnp.dot(comb[...], ep_in[box(s), :, at], preferred_element_type=jnp.float32)

    def straight(s, k):
        root, n, at = root_of(s), s - direct, within(s)
        held = s % acc.shape[0]
        if k == 0:

            @pl.when(z != root)
            def _():
                z_out[box(s), :, at] = acc[held, :, at].astype(jnp.bfloat16)
                slot = jnp.where(z < root, z, z - 1)
                remote(z_out.at[box(s), :, at], far_in.at[n, slot], z_s.at[s % 2], far_r.at[n],
                       (ep, root * 2 + core)).start()

        elif k == 1:

            @pl.when(z == root)
            def _():
                parts = far_in.at[n]
                remote(parts, parts, z_s.at[0], far_r.at[n], partner).wait_recv()
                total = acc[held, :, at]
                for slot in range(nz - 1):
                    total = total + far_in[n, slot].astype(jnp.float32)
                finish(s, total)
                here = out_ref.at[:, cols(core, s)]
                for other in range(1, nz):
                    remote(here, here, far_s.at[s % 2], b_r.at[s], (ep, ((root + other) % nz) * 2 + core)).start()
                to_partner(s).start()

        else:

            @pl.when(z != root)
            def _():
                outward(s, 0).wait_recv()
                to_partner(s).start()

    def chain(s, k, at_end=False):
        root = root_of(s)
        held = s % acc.shape[0]
        if k < top:

            @pl.when(((z < root) & (z == k)) | ((z > root) & (nz - 1 - z == k)))
            def _():
                total = acc[held]
                if k > 0:
                    side = jnp.where(z < root, 0, 1)
                    from_side(s, side).wait_recv()
                    total = total + z_in[s, side].astype(jnp.float32)
                z_out[box(s)] = total.astype(jnp.bfloat16)
                inward(s, root).start()

        elif k == top:

            @pl.when(z == root)
            def _():
                total = acc[held]
                for side in range(2):
                    from_side(s, side).wait_recv()
                    total = total + z_in[s, side].astype(jnp.float32)
                finish(s, total)
                outward(s, 0).start()
                outward(s, 1).start()
                to_partner(s).start()

        else:
            away = k - top

            end = (z == 0) | (z == nz - 1)

            @pl.when(((z == root - away) | (z == root + away)) & (end if at_end else jnp.logical_not(end)))
            def _():
                outward(s, 0).wait_recv()

                @pl.when((z < root) & (z > 0))
                def _():
                    outward(s, 0).start()

                @pl.when((z > root) & (z < nz - 1))
                def _():
                    outward(s, 1).start()

                to_partner(s).start()

    due = []
    landed = 4.5
    finish_at = landed + link * half / sub
    for s in range(steps):
        landed += link * widths[s] / sub
        due.append((max(0.01 * s, landed - 14.0), down, (s,)))
        due.append((landed, combine, (s,)))
        if s < direct:
            for k in range(2 * top + 1):
                due.append((landed + 0.1 + 3.6 * k, chain, (s, k)))
                if k > top:
                    late = landed + 0.1 + 3.6 * k + 4
                    due.append((late if late < finish_at - 2 else max(late, finish_at + 0.2), chain, (s, k, True)))
        else:
            for k in range(3):
                due.append((landed + 0.1 + 5.0 * k, straight, (s, k)))
    for _, action, given in sorted(due, key=lambda event: event[0]):
        with jax.named_scope(action.__name__ + "_".join(str(x) for x in given)):
            action(*given)

    mine_half = out_ref.at[:, pl.ds(0, half)]
    handed = remote(mine_half, mine_half, gfw_s.at[0], gfw_r.at[0], partner)
    with jax.named_scope("partner_recv"):
        handed.wait_recv()
    with jax.named_scope("sends"):
        handed.wait_send()
        full = pl.ds(0, half // sub)
        remote(ep_out.at[full], ep_out.at[full], ep_s.at[0], ep_r.at[0], partner).wait_send()
        remote(pair_out.at[full], pair_out.at[full], pair_s.at[0], pair_r.at[0], partner).wait_send()
        shared = rows.at[pl.ds(1, n_ep - 1), :, pl.ds(0, groups * sub)]
        remote(shared, shared, share_s.at[0], share_r.at[0], partner).wait_send()
        passed = rows.at[pl.ds(1, n_ep - 1), :, pl.ds(0, half)]
        remote(passed, passed, fwd_s.at[0], fwd_r.at[0, 0], partner).wait_send()
        chained = out_ref.at[:, pl.ds(0, sum(widths[:direct]) // 2)]
        spread = out_ref.at[:, pl.ds(0, sum(widths[direct:]) // 2 * (nz - 1))]
        for parity in range(2):
            root = root_of(parity)

            @pl.when(z != root)
            def _():
                sums = z_out.at[pl.ds(0, half // sub // 2)]
                remote(sums, sums, z_s.at[parity], z_r.at[0, 0], partner).wait_send()

            @pl.when(z == root)
            def _():
                remote(spread, spread, far_s.at[parity], b_r.at[0], partner).wait_send()

            @pl.when((z <= root) & (z > 0))
            def _():
                remote(chained, chained, b_s.at[parity, 0], b_r.at[0], partner).wait_send()

            @pl.when((z >= root) & (z < nz - 1))
            def _():
                remote(chained, chained, b_s.at[parity, 1], b_r.at[0], partner).wait_send()


def shards(n_ep, n_tp, tokens, expert_ids, router, gate_weight, up_weight, down_weight, keep_mask):
    experts = router.shape[1]
    toks, width = tokens.shape
    cap = 3 * toks // experts
    nz = n_tp // 2
    total = experts * cap
    sub = 256
    groups = width // 2 // sub // 3
    boxes = width // 2 // sub
    steps, far = len(chunk_widths(width // 2, sub)), 4
    w_gate, w_up, w_down = gate_weight[0], up_weight[0], down_weight[0]
    ff = w_gate.shape[1]
    vmem, hbm = pl.BlockSpec(memory_space=pltpu.VMEM), pl.BlockSpec(memory_space=pl.ANY)
    bf = jnp.bfloat16
    dma = pltpu.SemaphoreType.DMA
    return pl.pallas_call(
        functools.partial(kernel, n_ep, nz),
        out_shape=pltpu.VMEM((toks, width), bf),
        in_specs=[vmem, vmem, hbm, hbm, hbm, hbm, hbm],
        out_specs=vmem,
        scratch_shapes=[
            pltpu.VMEM((toks, width), bf),
            pltpu.VMEM((width, ff), bf), pltpu.VMEM((width, ff), bf), pltpu.VMEM((ff, width), bf),
            pltpu.VMEM((toks, width // 4), jnp.int32),
            pltpu.VMEM((experts, cap, width), bf),
            pltpu.VMEM((2, total, ff), jnp.float32),
            pltpu.VMEM((total, ff), bf),
            pltpu.VMEM((toks, total), bf),
            pltpu.VMEM((boxes, total, sub), bf), pltpu.VMEM((boxes, total, sub), bf),
            pltpu.VMEM((2, total, sub), bf),
            pltpu.VMEM((boxes, total - cap, sub), bf), pltpu.VMEM((boxes, total, sub), bf),
            pltpu.VMEM((boxes, toks, sub), bf), pltpu.VMEM((steps - far, 2, toks, sub), bf),
            pltpu.VMEM((far, nz - 1, toks, sub // 2), bf),
            pltpu.VMEM((8 if nz <= 4 else 10, toks, sub), jnp.float32),
            dma((3,)), dma((groups,)),
            dma((1,)), dma((2, groups)), dma((1,)), dma((groups,)), dma((1,)), dma((3, groups)),
            dma((1,)), dma((steps,)), dma((1,)), dma((steps,)),
            dma((2,)), dma((steps - far, 2)), dma((2,)), dma((far,)), dma((2, 2)), dma((steps,)),
            dma((1,)), dma((1,)),
        ],
        compiler_params=pltpu.CompilerParams(
            collective_id=0, has_side_effects=True, vmem_limit_bytes=65200000),
    )(expert_ids.T, router.T, tokens, w_gate, w_up, w_down, keep_mask)


def solution(mesh):
    return jax.shard_map(
        functools.partial(shards, mesh.shape["ep"], mesh.shape["tp"]),
        mesh=mesh,
        in_specs=(
            P("ep", None),
            P("ep", None),
            P(),
            P("ep", None, "tp"),
            P("ep", None, "tp"),
            P("ep", "tp", None),
            P("ep", None),
        ),
        out_specs=P("ep", None),
        check_vma=False,
    )
```

time: 82.3 us -> 77 us (0.936)
  Pallas kernels: 79.4 us -> 75.6 us
  local copies, waits for them, and re-layouts: 2.69 us -> 1.15 us
    pallas_call x1, Pallas kernels: 79.4 us -> 75.6 us  [shards(): pl.pallas_call(functools.partial(kernel, n_ep, nz), out_shape=pltpu.VMEM(...]
    unnamed x1, local copies, waits for them, and re-layouts: 2.69 us -> 1.15 us
where the time goes in v3:
time: 77 us; the launch traced here: 76.8 us
  Pallas kernels  75.6 us (98%)
  local copies, waits for them, and re-layouts  1.15 us (1%)
    pallas_call x1, Pallas kernels, shards(): pl.pallas_call(functools.partial(kernel, n_ep, nz), out_shape=pltpu.VMEM(...  75.6 us

profile of v3, /device:TPU:0, one launch (start us, length us, event | category | flops | bytes accessed | tf_op | source)
XLA Modules:
  0.0 76.8 jit_solution(953185527263006810)
XLA Ops:
  0.0 75.6 %shard_map.73 = bf16[128,6144]{1,0:T(8,128)(2,1)S(1)} custom-call(s32[2,128]{1,0:T(2,128)} %bitcast.9, bf16[4,6144]{1,0:T(4,128)(2,1)} %bitcast.8, bf16[128,6144]{1,0:T(8,128)(2,1)} %tokens_hbm.1, bf16[6144,1024]{1,0:T(8,128)(2,1)} %bitcast.5, bf16[6144,1024]{1,0:T(8,128)(2,1)} %bitcast.6, bf16[1024,6144]{1,0:T(8,128)(2,1)} %bitcast.7, s32[128,6144]{1,0:T(8,128)} %mask_hbm.1), custom_call_target="tpu_custom_call" | custom-call | tf_op jit(solution)/shard_map/pallas_call | solution.py:449
  75.6 1.1 %copy.9 = bf16[128,6144]{1,0:T(8,128)(2,1)} copy(bf16[128,6144]{1,0:T(8,128)(2,1)S(1)} %shard_map.73) | data formatting | bytes 3145728

commit v4 on v3

--- a/solution.py
+++ b/solution.py
@@ -19,7 +19,7 @@
 
 
 def chunk_widths(half, sub):
-    return [sub] * (half // sub - 2) + [sub // 2] * 4
+    return [sub] * (half // sub - 4) + [sub // 2] * 8
 
 
 def kernel(
@@ -136,10 +136,10 @@
             share(g).start()
         forward(kind, g).start()
 
-    order = [(0, 0)]
+    order = [(0, g) for g in range(2)]
     for g in range(groups):
-        if g + 1 < groups:
-            order.append((0, g + 1))
+        if g + 2 < groups:
+            order.append((0, g + 2))
         order.append((1, g))
     with jax.named_scope("tokens"):
         load_tokens.wait()
@@ -212,7 +212,7 @@
             loaded.add(g)
             wait_weights(g)
 
-    link, share_link, hop, cross, unit = 2.26, 3.4, 1.8, 1.4, 2.3
+    link, share_link, hop, cross, unit = 2.26, 3.4, 3.0, 1.4, 2.3
     passes, busy = [], 0.0
     for n, (kind, g) in enumerate(order):
         landed = link * (n + 1) + hop
@@ -271,10 +271,13 @@
     def inward(s, root):
         side = jnp.where(z < root, 0, 1)
         to = jnp.where(z < root, z + 1, z - 1)
-        return remote(z_out.at[box(s)], z_in.at[s, side], z_s.at[s % 2], z_r.at[s, side], (ep, to * 2 + core))
+        at = within(s)
+        return remote(z_out.at[box(s), :, at], z_in.at[s, side, :, at], z_s.at[s % 2], z_r.at[s, side],
+                      (ep, to * 2 + core))
 
     def from_side(s, side):
-        return remote(z_out.at[box(s)], z_in.at[s, side], z_s.at[s % 2], z_r.at[s, side], partner)
+        at = within(s)
+        return remote(z_out.at[box(s), :, at], z_in.at[s, side, :, at], z_s.at[s % 2], z_r.at[s, side], partner)
 
     def outward(s, side):
         here = out_ref.at[:, cols(core, s)]
@@ -330,27 +333,27 @@
 
     def chain(s, k, at_end=False):
         root = root_of(s)
-        held = s % acc.shape[0]
+        held, at = s % acc.shape[0], within(s)
         if k < top:
 
             @pl.when(((z < root) & (z == k)) | ((z > root) & (nz - 1 - z == k)))
             def _():
-                total = acc[held]
+                total = acc[held, :, at]
                 if k > 0:
                     side = jnp.where(z < root, 0, 1)
                     from_side(s, side).wait_recv()
-                    total = total + z_in[s, side].astype(jnp.float32)
-                z_out[box(s)] = total.astype(jnp.bfloat16)
+                    total = total + z_in[s, side, :, at].astype(jnp.float32)
+                z_out[box(s), :, at] = total.astype(jnp.bfloat16)
                 inward(s, root).start()
 
         elif k == top:
 
             @pl.when(z == root)
             def _():
-                total = acc[held]
+                total = acc[held, :, at]
                 for side in range(2):
                     from_side(s, side).wait_recv()
-                    total = total + z_in[s, side].astype(jnp.float32)
+                    total = total + z_in[s, side, :, at].astype(jnp.float32)
                 finish(s, total)
                 outward(s, 0).start()
                 outward(s, 1).start()
@@ -464,7 +467,7 @@
             pltpu.VMEM((boxes, total - cap, sub), bf), pltpu.VMEM((boxes, total, sub), bf),
             pltpu.VMEM((boxes, toks, sub), bf), pltpu.VMEM((steps - far, 2, toks, sub), bf),
             pltpu.VMEM((far, nz - 1, toks, sub // 2), bf),
-            pltpu.VMEM((8 if nz <= 4 else 10, toks, sub), jnp.float32),
+            pltpu.VMEM((8 if nz <= 4 else 12, toks, sub), jnp.float32),
             dma((3,)), dma((groups,)),
             dma((1,)), dma((2, groups)), dma((1,)), dma((groups,)), dma((1,)), dma((3, groups)),
             dma((1,)), dma((steps,)), dma((1,)), dma((steps,)),

time: 77 us -> 75.4 us (0.979)
  Pallas kernels: 75.6 us -> 74.1 us
    pallas_call x1, Pallas kernels: 75.6 us -> 74.1 us  [shards(): pl.pallas_call(functools.partial(kernel, n_ep, nz), out_shape=pltpu.VMEM(...]
where the time goes in v4:
time: 75.4 us; the launch traced here: 75.2 us
  Pallas kernels  74.1 us (98%)
  local copies, waits for them, and re-layouts  1.15 us (2%)
    pallas_call x1, Pallas kernels, shards(): pl.pallas_call(functools.partial(kernel, n_ep, nz), out_shape=pltpu.VMEM(...  74.1 us

profile of v4, /device:TPU:0, one launch (start us, length us, event | category | flops | bytes accessed | tf_op | source)
XLA Modules:
  0.0 75.2 jit_solution(17996874290548642514)
XLA Ops:
  0.0 74.1 %shard_map.73 = bf16[128,6144]{1,0:T(8,128)(2,1)S(1)} custom-call(s32[2,128]{1,0:T(2,128)} %bitcast.9, bf16[4,6144]{1,0:T(4,128)(2,1)} %bitcast.8, bf16[128,6144]{1,0:T(8,128)(2,1)} %tokens_hbm.1, bf16[6144,1024]{1,0:T(8,128)(2,1)} %bitcast.5, bf16[6144,1024]{1,0:T(8,128)(2,1)} %bitcast.6, bf16[1024,6144]{1,0:T(8,128)(2,1)} %bitcast.7, s32[128,6144]{1,0:T(8,128)} %mask_hbm.1), custom_call_target="tpu_custom_call" | custom-call | tf_op jit(solution)/shard_map/pallas_call | solution.py:452
  74.1 1.1 %copy.9 = bf16[128,6144]{1,0:T(8,128)(2,1)} copy(bf16[128,6144]{1,0:T(8,128)(2,1)S(1)} %shard_map.73) | data formatting | bytes 3145728
